TPU v7x, 32 devices: a whole 2x2x4 slice. The times are simulated.
32 devices in a mesh: dp: 8 (over z, x), param: 4 (over y, core).
Axes of the slice: x: 2, y: 2, z: 4, core: 2. Of those that a mesh axis runs over, the one named last changes fastest.
Arguments:
- ex_grads: bfloat16 [768, 5120], P('dp', 'param'), may hold values from -6 to 6
- tgt_grads: bfloat16 [2048, 5120], P('dp', 'param'), may hold values from -6 to 6
- projection: bfloat16 [5120, 4096], P('param'), may hold values from -0.078125 to 0.078125
- example_weight: float32 [768], P('param'), may hold values from 0.05 to 1
Outputs:
- scores: float32 [2048, 768], P('dp', 'param')
All inputs are finite; a program needn't handle non-finite values.
Results may differ from a plain program's by a relative error of at most 0.0078.
Values may be sent and summed in bfloat16 or wider, within the bound.
A program may use at most 192 MiB of HBM per device.

v0:
```python
import math
import jax
import jax.numpy as jnp
from jax import lax
from jax.sharding import PartitionSpec as P

ridge_value = 0.5


def with_ridge(block, first_row):
    row_ids = lax.broadcasted_iota(jnp.int32, block.shape, 0) + first_row
    col_ids = lax.broadcasted_iota(jnp.int32, block.shape, 1)
    return block + jnp.where(row_ids == col_ids, ridge_value, 0.0).astype(jnp.float32)


def on_device(ex_grads, tgt_grads, projection, example_weight):
    ex_rows = ex_grads.shape[0]
    columns = projection.shape[1]
    param_total = lax.axis_size("param")
    param_pos = lax.axis_index("param")
    replica_pos = lax.axis_index("dp")
    stacked = jnp.concatenate([ex_grads, tgt_grads], axis=0)
    contract_rows = (((0,), (1,)), ((), ()))
    feature_block = lax.psum_scatter(
        lax.dot_general(projection, stacked, contract_rows, preferred_element_type=jnp.float32),
        "param",
        scatter_dimension=0,
        tiled=True,
    )
    local_features = feature_block.astype(jnp.bfloat16)
    example_part = local_features[:, :ex_rows]
    contract_first = (((0,), (0,)), ((), ()))
    partial_value = lax.dot_general(
        local_features,
        lax.all_gather(example_part, "dp", axis=1, tiled=True),
        contract_first,
        preferred_element_type=jnp.float32,
    )
    examples = partial_value.shape[1]
    summed = lax.psum(partial_value, "param")
    kernel_block = with_ridge(summed[:ex_rows] / columns, replica_pos * ex_rows)
    kernel = lax.all_gather(kernel_block, "dp", axis=0, tiled=True)
    cross_terms = summed[ex_rows:] / columns
    factor = jnp.linalg.cholesky(kernel)
    forward = jax.scipy.linalg.solve_triangular(factor, cross_terms.T, lower=True)
    solved = jax.scipy.linalg.solve_triangular(factor, forward, lower=True, trans=1)
    block_cols = examples // param_total
    chosen = lax.dynamic_slice_in_dim(solved.T, param_pos * block_cols, block_cols, 1)
    return chosen * math.sqrt(columns) * example_weight[None, :]


def solution(mesh):
    placed = (P("dp", "param"), P("dp", "param"), P("param", None), P("param"))
    return jax.shard_map(
        on_device, mesh=mesh, in_specs=placed, out_specs=P("dp", "param"), check_vma=False
    )
```

profile of v0, /device:TPU:0, one launch (start us, length us, event | category | flops | bytes accessed | tf_op | source)
XLA Modules:
  0.0 462.6 jit_solution(8862410163447170017)
XLA Ops:
  6.5 10.7 %convolution_bitcast_fusion = f32[4096,352]{0,1:T(8,128)} fusion(bf16[1280,4096]{1,0:T(8,128)(2,1)} %param.6, bf16[256,1280]{1,0:T(8,128)(2,1)} %param.5, bf16[96,1280]{1,0:T(8,128)(2,1)} %param.4), kind=kOutput, calls=%fused_computation.2 | convolution fusion | flops 3692789760 | bytes 17154048 | tf_op jit(solution)/shard_map/dot_general | solution.py:25
  17.3 57.3 %reduce-scatter.2.cloned.1.call-done = f32[1024,352]{0,1:T(8,128)} async-done(((f32[4096,352]{0,1:T(8,128)}), f32[1024,352]{0,1:T(8,128)}) %reduce-scatter.2.cloned.1.call-update) | async-done | bytes 1441808 | tf_op jit(solution)/shard_map/reduce_scatter | solution.py:24
  74.6 1.5 convert_element_type.3
  76.1 0.7 slice.254
  76.9 44.3 %all-gather.3.cloned.1.call-done = bf16[1024,768]{0,1:T(8,128)(2,1)} async-done(((bf16[1024,96]{0,1:T(8,128)(2,1)}), bf16[1024,768]{0,1:T(8,128)(2,1)}) %all-gather.3.cloned.1.call-update) | async-done | bytes 1572880 | tf_op jit(solution)/shard_map/all_gather | solution.py:35
  121.2 3.2 fusion.85
  124.4 35.1 %all-reduce.3.cloned.1.call-done = f32[352,768]{1,0:T(8,128)} async-done(((f32[352,768]{1,0:T(8,128)}), f32[352,768]{1,0:T(8,128)}) %all-reduce.3.cloned.1.call-update) | async-done | bytes 1081360 | tf_op jit(solution)/shard_map/psum | solution.py:40
  159.6 1.8 fusion.37
  161.4 0.6 iota_multiply_fusion
  162.0 1.2 fusion.4
  163.2 50.6 %all-gather.5.cloned.1.call-done = f32[768,768]{1,0:T(8,128)} async-done(((f32[96,768]{1,0:T(8,128)}), f32[768,768]{1,0:T(8,128)}) %all-gather.5.cloned.1.call-update) | async-done | bytes 2359312 | tf_op jit(solution)/shard_map/all_gather | solution.py:42
  213.8 3.3 copy.7
  217.1 2.0 fusion
  219.1 1.4 copy-done.2
  220.5 11.7 %cholesky.165 = f32[128,128]{1,0:T(8,128)S(1)} custom-call(f32[128,128]{1,0:T(8,128)S(1)} %cholesky.424), custom_call_target="Cholesky" | custom-call | tf_op jit(solution)/shard_map/jit(cholesky)/cholesky | solution.py:44
  232.4 9.8 %custom-call.50 = f32[1,128,128]{1,2,0:T(8,128)S(1)} custom-call(f32[1,128,128]{2,1,0:T(8,128)S(1)} %get-tuple-element.38), custom_call_target="InvertDiagBlocksLowerTriangular" | custom-call | tf_op jit(solution)/shard_map/jit(cholesky)/cholesky | solution.py:44
  242.2 1.4 constant_dynamic-update-slice_fusion.20
  243.6 1.4 convolution_subtract_fusion
  245.0 0.6 cholesky.428
  245.7 12.5 %cholesky.188 = f32[128,128]{1,0:T(8,128)S(1)} custom-call(f32[128,128]{1,0:T(8,128)} %cholesky.428), custom_call_target="Cholesky" | custom-call | tf_op jit(solution)/shard_map/jit(cholesky)/cholesky | solution.py:44
  258.2 0.6 select_reduce_fusion.4
  258.9 10.8 %custom-call.51 = f32[1,128,128]{1,2,0:T(8,128)S(1)} custom-call(f32[1,128,128]{2,1,0:T(8,128)} %get-tuple-element.35), custom_call_target="InvertDiagBlocksLowerTriangular" | custom-call | tf_op jit(solution)/shard_map/jit(cholesky)/cholesky | solution.py:44
  269.7 0.4 convolution_dynamic-update-slice_fusion
  270.1 1.5 convolution_subtract_fusion.1
  271.6 11.7 %cholesky.354 = f32[128,128]{1,0:T(8,128)S(1)} custom-call(f32[128,128]{1,0:T(8,128)S(1)} %cholesky.433), custom_call_target="Cholesky" | custom-call | tf_op jit(solution)/shard_map/jit(cholesky)/cholesky | solution.py:44
  283.4 9.8 %custom-call.52 = f32[1,128,128]{1,2,0:T(8,128)S(1)} custom-call(f32[1,128,128]{2,1,0:T(8,128)S(1)} %get-tuple-element.32), custom_call_target="InvertDiagBlocksLowerTriangular" | custom-call | tf_op jit(solution)/shard_map/jit(cholesky)/cholesky | solution.py:44
  293.5 1.6 convolution_subtract_fusion.2
  295.1 12.1 %cholesky.373 = f32[128,128]{1,0:T(8,128)S(1)} custom-call(f32[128,128]{1,0:T(8,128)S(1)} %cholesky.438), custom_call_target="Cholesky" | custom-call | tf_op jit(solution)/shard_map/jit(cholesky)/cholesky | solution.py:44
  307.3 9.8 %custom-call.53 = f32[1,128,128]{1,2,0:T(8,128)S(1)} custom-call(f32[1,128,128]{2,1,0:T(8,128)S(1)} %get-tuple-element.29), custom_call_target="InvertDiagBlocksLowerTriangular" | custom-call | tf_op jit(solution)/shard_map/jit(cholesky)/cholesky | solution.py:44
  317.4 1.5 convolution_subtract_fusion.11
  318.9 11.7 %cholesky.392 = f32[128,128]{1,0:T(8,128)S(1)} custom-call(f32[128,128]{1,0:T(8,128)S(1)} %cholesky.443), custom_call_target="Cholesky" | custom-call | tf_op jit(solution)/shard_map/jit(cholesky)/cholesky | solution.py:44
  330.6 9.8 %custom-call.54 = f32[1,128,128]{1,2,0:T(8,128)S(1)} custom-call(f32[1,128,128]{2,1,0:T(8,128)S(1)} %get-tuple-element.26), custom_call_target="InvertDiagBlocksLowerTriangular" | custom-call | tf_op jit(solution)/shard_map/jit(cholesky)/cholesky | solution.py:44
  340.6 1.3 convolution_subtract_fusion.14
  342.0 11.9 %cholesky.410 = f32[128,128]{1,0:T(8,128)S(1)} custom-call(f32[128,128]{1,0:T(8,128)S(1)} %convolution_subtract_fusion.14), custom_call_target="Cholesky" | custom-call | tf_op jit(solution)/shard_map/jit(cholesky)/cholesky | solution.py:44
  353.9 0.7 compare_reduce_fusion.3
  354.6 0.6 compare_reduce_fusion.2
  355.2 0.7 compare_reduce_fusion.1
  355.9 0.7 compare_reduce_fusion
  356.6 0.7 compare_reduce_fusion.4
  361.0 1.6 select_select_fusion
  362.6 20.5 %while.1 = (s32[]{:T(128)}, f32[768,768]{1,0:T(8,128)}, s32[6,2]{0,1:T(2,128)S(1)}, f32[6,128,128]{2,1,0:T(8,128)}, s32[]{:T(128)}) while((s32[]{:T(128)}, f32[768,768]{1,0:T(8,128)}, s32[6,2]{0,1:T(2,128)S(1)}, f32[6,128,128]{2,1,0:T(8,128)}, s32[]{:T(128)}) %tuple.37), condition=%wide.while_cond, body=%wide.while_body.sunk | while | flops 2 | bytes 132205 | solution.py:46
  362.7 0.5 fusion.106
  363.2 2.8 bitcast_dynamic-update-slice_fusion.2
  366.1 0.5 fusion.106
  366.6 2.8 bitcast_dynamic-update-slice_fusion.2
  369.5 0.5 fusion.106
  370.1 2.8 bitcast_dynamic-update-slice_fusion.2
  372.9 0.5 fusion.106
  373.5 2.8 bitcast_dynamic-update-slice_fusion.2
  376.4 0.5 fusion.106
  376.9 2.8 bitcast_dynamic-update-slice_fusion.2
  379.8 0.5 fusion.106
  380.3 2.8 bitcast_dynamic-update-slice_fusion.2
  383.1 59.9 %custom-call.55 = f32[6,128,128]{1,2,0:T(8,128)S(1)} custom-call(f32[6,128,128]{2,1,0:T(8,128)} %get-tuple-element.12), custom_call_target="InvertDiagBlocksLowerTriangular" | custom-call | tf_op jit(solution)/shard_map/jit(_solve_triangular)/triangular_solve | solution.py:46
  443.3 1.2 convolution_subtract_fusion.13
  444.9 1.5 convolution_subtract_fusion.10
  446.7 0.8 convolution_subtract_fusion.9
  447.8 1.0 convolution_subtract_fusion.8
  449.2 1.3 convolution_subtract_fusion.7
  451.6 0.4 convolution_subtract_fusion.6
  452.3 0.5 convolution_subtract_fusion.5
  453.1 0.6 convolution_subtract_fusion.4
  454.0 0.7 convolution_subtract_fusion.3
  455.1 0.8 multiply_bitcast_fusion
  (62 shorter events, 5.6 us)
Async XLA Ops:
  6.5 68.1 %reduce-scatter.2.cloned.1.call-start = ((), (), s32[]{:S(2)}) async-start(), calls=%async_computation.1 | async-start | bytes 7208960 | tf_op jit(solution)/shard_map/reduce_scatter | solution.py:24
  17.2 103.9 %all-gather.3.cloned.1.call-start = ((), (), s32[]{:S(2)}) async-start(), calls=%async_computation.2 | async-start | bytes 1769472 | tf_op jit(solution)/shard_map/all_gather | solution.py:35
  76.8 85.2 %copy-start.3 = (f32[192]{0:T(256)S(1)}, f32[192]{0:T(256)}, u32[]{:S(2)}) copy-start(f32[192]{0:T(256)} %param.7) | copy-start | bytes 2308
  76.8 82.7 %all-reduce.3.cloned.1.call-start = ((), (), s32[]{:S(2)}) async-start(), calls=%async_computation.3 | async-start | bytes 2162688 | tf_op jit(solution)/shard_map/psum | solution.py:40
  124.4 89.4 %all-gather.5.cloned.1.call-start = ((), (), s32[]{:S(2)}) async-start(), calls=%async_computation.4 | async-start | bytes 2654208 | tf_op jit(solution)/shard_map/all_gather | solution.py:42
  213.8 3.3 copy-start
  219.1 1.4 copy-start.2
  361.0 1.6 copy-start.4
  383.1 63.6 %copy-start.1 = (f32[768,768]{1,0:T(8,128)S(1)}, f32[768,768]{1,0:T(8,128)}, u32[]{:S(2)}) copy-start(f32[768,768]{1,0:T(8,128)} %get-tuple-element.104) | copy-start | bytes 7077892
Sparse Core Ops, SparseCore 0:
  17.4 57.2 reduce-scatter.1
  77.0 44.1 all-gather.2
  124.5 35.0 all-reduce.2
  161.6 52.1 all-gather.4
where the time goes:
time: 467 us; the launch traced here: 463 us
  other arithmetic  195 us (42%)
  waiting for transfers between devices  187 us (40%)
  matrix products  35.5 us (8%)
  local copies, waits for them, and re-layouts  26.8 us (6%)
  between operations  17.6 us (4%)
    another operation x22, other arithmetic, on_device(): factor = jnp.linalg.cholesky(kernel)  126 us
    another operation x3, other arithmetic, on_device(): jax.scipy.linalg.solve_triangular(factor, forward, lower=True, trans=1)  62.1 us
    reduce_scatter x1, waiting for transfers between devices, on_device(): lax.psum_scatter(lax.dot_general(projection, stacked, contract_rows, pref...  57.3 us
    all_gather x1, waiting for transfers between devices, on_device(): kernel = lax.all_gather(kernel_block, 'dp', axis=0, tiled=True)  50.6 us
    all_gather x1, waiting for transfers between devices, on_device(): lax.all_gather(example_part, 'dp', axis=1, tiled=True)  44.3 us
    psum x1, waiting for transfers between devices, on_device(): summed = lax.psum(partial_value, 'param')  35.1 us
    another operation x18, local copies, waits for them, and re-layouts  20.4 us
    dot_general x1, matrix products, on_device(): lax.dot_general(projection, stacked, contract_rows, preferred_element_typ...  10.7 us
  transfers between devices with their start and end apart: 4, of which 4 were waited for; matrix products, arithmetic and copies ran while one was open for 0% of the time, Pallas kernels for 0%

commit v1 on v0

--- a/solution.py
+++ b/solution.py
@@ -30,9 +30,13 @@
     local_features = feature_block.astype(jnp.bfloat16)
     example_part = local_features[:, :ex_rows]
     contract_first = (((0,), (0,)), ((), ()))
+
+    def create_the_pieces_all(local_values):
+        return jnp.concatenate(lax.all_gather(local_values, "dp"), axis=1)
+
     partial_value = lax.dot_general(
         local_features,
-        lax.all_gather(example_part, "dp", axis=1, tiled=True),
+        create_the_pieces_all(example_part),
         contract_first,
         preferred_element_type=jnp.float32,
     )

time: 467 us -> 467 us (level)
  no operation moved by 1% of the time
where the time goes in v1:
time: 467 us; the launch traced here: 463 us
  other arithmetic  195 us (42%)
  waiting for transfers between devices  187 us (40%)
  matrix products  34.1 us (7%)
  local copies, waits for them, and re-layouts  28.4 us (6%)
  between operations  17.6 us (4%)
    another operation x22, other arithmetic, on_device(): factor = jnp.linalg.cholesky(kernel)  126 us
    another operation x3, other arithmetic, on_device(): jax.scipy.linalg.solve_triangular(factor, forward, lower=True, trans=1)  62.1 us
    reduce_scatter x1, waiting for transfers between devices, on_device(): lax.psum_scatter(lax.dot_general(projection, stacked, contract_rows, pref...  57.3 us
    all_gather x1, waiting for transfers between devices, on_device(): kernel = lax.all_gather(kernel_block, 'dp', axis=0, tiled=True)  50.6 us
    all_gather x1, waiting for transfers between devices, create_the_pieces_all(): return jnp.concatenate(lax.all_gather(local_values, 'dp'), axis=1)  44.3 us
    psum x1, waiting for transfers between devices, on_device(): summed = lax.psum(partial_value, 'param')  35.1 us
    another operation x18, local copies, waits for them, and re-layouts  20.4 us
    dot_general x1, matrix products, on_device(): lax.dot_general(projection, stacked, contract_rows, preferred_element_typ...  10.7 us
  transfers between devices with their start and end apart: 4, of which 4 were waited for; matrix products, arithmetic and copies ran while one was open for 0% of the time, Pallas kernels for 0%

profile of v1, /device:TPU:0, one launch (start us, length us, event | category | flops | bytes accessed | tf_op | source)
XLA Modules:
  0.0 462.8 jit_solution(10278791231557910034)
XLA Ops:
  6.5 10.7 %convolution_bitcast_fusion = f32[4096,352]{0,1:T(8,128)} fusion(bf16[1280,4096]{1,0:T(8,128)(2,1)} %param.6, bf16[256,1280]{1,0:T(8,128)(2,1)} %param.5, bf16[96,1280]{1,0:T(8,128)(2,1)} %param.4), kind=kOutput, calls=%fused_computation.2 | convolution fusion | flops 3692789760 | bytes 17154048 | tf_op jit(solution)/shard_map/dot_general | solution.py:25
  17.3 57.3 %reduce-scatter.2.cloned.1.call-done = f32[1024,352]{0,1:T(8,128)} async-done(((f32[4096,352]{0,1:T(8,128)}), f32[1024,352]{0,1:T(8,128)}) %reduce-scatter.2.cloned.1.call-update) | async-done | bytes 1441808 | tf_op jit(solution)/shard_map/reduce_scatter | solution.py:24
  74.6 1.5 convert_element_type.3
  76.1 0.7 slice.254
  76.9 44.3 %all-gather.6.cloned.1.call-done = bf16[8192,96]{0,1:T(8,128)(2,1)} async-done(((bf16[1024,96]{0,1:T(8,128)(2,1)}), bf16[8192,96]{0,1:T(8,128)(2,1)}) %all-gather.6.cloned.1.call-update) | async-done | bytes 1572880 | tf_op jit(solution)/shard_map/all_gather | solution.py:35
  121.2 1.5 copy.24
  122.7 1.8 fusion.85
  124.6 35.1 %all-reduce.3.cloned.1.call-done = f32[352,768]{1,0:T(8,128)} async-done(((f32[352,768]{1,0:T(8,128)}), f32[352,768]{1,0:T(8,128)}) %all-reduce.3.cloned.1.call-update) | async-done | bytes 1081360 | tf_op jit(solution)/shard_map/psum | solution.py:44
  159.7 1.8 fusion.37
  161.6 0.6 iota_multiply_fusion
  162.2 1.2 fusion.4
  163.4 50.6 %all-gather.4.cloned.1.call-done = f32[768,768]{1,0:T(8,128)} async-done(((f32[96,768]{1,0:T(8,128)}), f32[768,768]{1,0:T(8,128)}) %all-gather.4.cloned.1.call-update) | async-done | bytes 2359312 | tf_op jit(solution)/shard_map/all_gather | solution.py:46
  214.0 3.3 copy.11
  217.3 2.0 fusion
  219.3 1.4 copy-done.2
  220.7 11.7 %cholesky.165 = f32[128,128]{1,0:T(8,128)S(1)} custom-call(f32[128,128]{1,0:T(8,128)S(1)} %cholesky.424), custom_call_target="Cholesky" | custom-call | tf_op jit(solution)/shard_map/jit(cholesky)/cholesky | solution.py:48
  232.6 9.8 %custom-call.50 = f32[1,128,128]{1,2,0:T(8,128)S(1)} custom-call(f32[1,128,128]{2,1,0:T(8,128)S(1)} %get-tuple-element.38), custom_call_target="InvertDiagBlocksLowerTriangular" | custom-call | tf_op jit(solution)/shard_map/jit(cholesky)/cholesky | solution.py:48
  242.4 1.4 constant_dynamic-update-slice_fusion.20
  243.8 1.4 convolution_subtract_fusion
  245.2 0.6 cholesky.428
  245.8 12.5 %cholesky.188 = f32[128,128]{1,0:T(8,128)S(1)} custom-call(f32[128,128]{1,0:T(8,128)} %cholesky.428), custom_call_target="Cholesky" | custom-call | tf_op jit(solution)/shard_map/jit(cholesky)/cholesky | solution.py:48
  258.4 0.6 select_reduce_fusion.4
  259.0 10.8 %custom-call.51 = f32[1,128,128]{1,2,0:T(8,128)S(1)} custom-call(f32[1,128,128]{2,1,0:T(8,128)} %get-tuple-element.35), custom_call_target="InvertDiagBlocksLowerTriangular" | custom-call | tf_op jit(solution)/shard_map/jit(cholesky)/cholesky | solution.py:48
  270.3 1.5 convolution_subtract_fusion.1
  271.8 11.7 %cholesky.354 = f32[128,128]{1,0:T(8,128)S(1)} custom-call(f32[128,128]{1,0:T(8,128)S(1)} %cholesky.433), custom_call_target="Cholesky" | custom-call | tf_op jit(solution)/shard_map/jit(cholesky)/cholesky | solution.py:48
  283.6 9.8 %custom-call.52 = f32[1,128,128]{1,2,0:T(8,128)S(1)} custom-call(f32[1,128,128]{2,1,0:T(8,128)S(1)} %get-tuple-element.32), custom_call_target="InvertDiagBlocksLowerTriangular" | custom-call | tf_op jit(solution)/shard_map/jit(cholesky)/cholesky | solution.py:48
  293.7 1.6 convolution_subtract_fusion.2
  295.3 12.1 %cholesky.373 = f32[128,128]{1,0:T(8,128)S(1)} custom-call(f32[128,128]{1,0:T(8,128)S(1)} %cholesky.438), custom_call_target="Cholesky" | custom-call | tf_op jit(solution)/shard_map/jit(cholesky)/cholesky | solution.py:48
  307.4 9.8 %custom-call.53 = f32[1,128,128]{1,2,0:T(8,128)S(1)} custom-call(f32[1,128,128]{2,1,0:T(8,128)S(1)} %get-tuple-element.29), custom_call_target="InvertDiagBlocksLowerTriangular" | custom-call | tf_op jit(solution)/shard_map/jit(cholesky)/cholesky | solution.py:48
  317.5 1.5 convolution_subtract_fusion.11
  319.0 11.7 %cholesky.392 = f32[128,128]{1,0:T(8,128)S(1)} custom-call(f32[128,128]{1,0:T(8,128)S(1)} %cholesky.443), custom_call_target="Cholesky" | custom-call | tf_op jit(solution)/shard_map/jit(cholesky)/cholesky | solution.py:48
  330.8 9.8 %custom-call.54 = f32[1,128,128]{1,2,0:T(8,128)S(1)} custom-call(f32[1,128,128]{2,1,0:T(8,128)S(1)} %get-tuple-element.26), custom_call_target="InvertDiagBlocksLowerTriangular" | custom-call | tf_op jit(solution)/shard_map/jit(cholesky)/cholesky | solution.py:48
  340.8 1.3 convolution_subtract_fusion.14
  342.1 11.9 %cholesky.410 = f32[128,128]{1,0:T(8,128)S(1)} custom-call(f32[128,128]{1,0:T(8,128)S(1)} %convolution_subtract_fusion.14), custom_call_target="Cholesky" | custom-call | tf_op jit(solution)/shard_map/jit(cholesky)/cholesky | solution.py:48
  354.0 0.7 compare_reduce_fusion.3
  354.8 0.6 compare_reduce_fusion.2
  355.4 0.7 compare_reduce_fusion.1
  356.0 0.7 compare_reduce_fusion
  356.7 0.7 compare_reduce_fusion.4
  361.2 1.6 select_select_fusion
  362.8 20.5 %while.1 = (s32[]{:T(128)}, f32[768,768]{1,0:T(8,128)}, s32[6,2]{0,1:T(2,128)S(1)}, f32[6,128,128]{2,1,0:T(8,128)}, s32[]{:T(128)}) while((s32[]{:T(128)}, f32[768,768]{1,0:T(8,128)}, s32[6,2]{0,1:T(2,128)S(1)}, f32[6,128,128]{2,1,0:T(8,128)}, s32[]{:T(128)}) %tuple.37), condition=%wide.while_cond, body=%wide.while_body.sunk | while | flops 2 | bytes 132205 | solution.py:50
  362.9 0.5 fusion.106
  363.4 2.8 bitcast_dynamic-update-slice_fusion.2
  366.3 0.5 fusion.106
  366.8 2.8 bitcast_dynamic-update-slice_fusion.2
  369.7 0.5 fusion.106
  370.2 2.8 bitcast_dynamic-update-slice_fusion.2
  373.1 0.5 fusion.106
  373.6 2.8 bitcast_dynamic-update-slice_fusion.2
  376.5 0.5 fusion.106
  377.1 2.8 bitcast_dynamic-update-slice_fusion.2
  380.0 0.5 fusion.106
  380.5 2.8 bitcast_dynamic-update-slice_fusion.2
  383.2 59.9 %custom-call.55 = f32[6,128,128]{1,2,0:T(8,128)S(1)} custom-call(f32[6,128,128]{2,1,0:T(8,128)} %get-tuple-element.12), custom_call_target="InvertDiagBlocksLowerTriangular" | custom-call | tf_op jit(solution)/shard_map/jit(_solve_triangular)/triangular_solve | solution.py:50
  443.5 1.2 convolution_subtract_fusion.13
  445.0 1.5 convolution_subtract_fusion.10
  446.9 0.8 convolution_subtract_fusion.9
  448.0 1.0 convolution_subtract_fusion.8
  449.4 1.3 convolution_subtract_fusion.7
  451.8 0.4 convolution_subtract_fusion.6
  452.5 0.5 convolution_subtract_fusion.5
  453.2 0.6 convolution_subtract_fusion.4
  454.2 0.7 convolution_subtract_fusion.3
  455.3 0.8 multiply_bitcast_fusion
  (63 shorter events, 6.0 us)
Async XLA Ops:
  6.5 68.1 %reduce-scatter.2.cloned.1.call-start = ((), (), s32[]{:S(2)}) async-start(), calls=%async_computation.1 | async-start | bytes 7208960 | tf_op jit(solution)/shard_map/reduce_scatter | solution.py:24
  17.2 103.9 %all-gather.6.cloned.1.call-start = ((), (), s32[]{:S(2)}) async-start(), calls=%async_computation.4 | async-start | bytes 1769472 | tf_op jit(solution)/shard_map/all_gather | solution.py:35
  76.8 82.9 %all-reduce.3.cloned.1.call-start = ((), (), s32[]{:S(2)}) async-start(), calls=%async_computation.2 | async-start | bytes 2162688 | tf_op jit(solution)/shard_map/psum | solution.py:44
  122.7 39.4 %copy-start.3 = (f32[192]{0:T(256)S(1)}, f32[192]{0:T(256)}, u32[]{:S(2)}) copy-start(f32[192]{0:T(256)} %param.7) | copy-start | bytes 2308
  124.6 89.4 %all-gather.4.cloned.1.call-start = ((), (), s32[]{:S(2)}) async-start(), calls=%async_computation.3 | async-start | bytes 2654208 | tf_op jit(solution)/shard_map/all_gather | solution.py:46
  214.0 3.3 copy-start
  219.3 1.4 copy-start.2
  361.2 1.6 copy-start.4
  383.2 63.6 %copy-start.1 = (f32[768,768]{1,0:T(8,128)S(1)}, f32[768,768]{1,0:T(8,128)}, u32[]{:S(2)}) copy-start(f32[768,768]{1,0:T(8,128)} %get-tuple-element.104) | copy-start | bytes 7077892
Sparse Core Ops, SparseCore 0:
  17.4 57.2 reduce-scatter.1
  77.0 44.1 all-gather.5
  124.7 35.0 all-reduce.2
  161.8 52.1 all-gather.3
